TPU v7x, 512 devices: a whole 4x8x8 slice. The times are simulated.
512 devices in a mesh: section: 8 (over z_hi, core), dp: 64 (over y, x, z_lo).
Axes of the slice: x: 4, y: 8, z: 8 (z_hi: 4, z_lo: 2; z = z_hi * 2 + z_lo), core: 2. Of those that a mesh axis runs over, the one named last changes fastest.
Arguments:
- tokens: bfloat16 [2, 64, 80, 1024], P(None, 'dp'), may hold values from -6 to 6
- w_qkv: bfloat16 [8, 1024, 1536], P('section', 'dp'), may hold values from -0.1875 to 0.1875
- w_output: bfloat16 [8, 512, 1024], P('section', None, 'dp'), may hold values from -0.25 to 0.25
- tangent_value: bfloat16 [8, 2, 1024, 512], P('section', None, 'dp'), may hold values from -0.1875 to 0.1875
- tangent_output: bfloat16 [8, 2, 512, 1024], P('section', None, None, 'dp'), may hold values from -0.25 to 0.25
- layer_gain: float32 [8, 1024], P('section'), may hold values from 0.5 to 1.5
- final_gain: float32 [1024], replicated, may hold values from 0.5 to 1.5
- head: bfloat16 [1024, 1000], P(None, 'section'), may hold values from -0.1875 to 0.1875
Outputs:
- mean_logits: float32 [2, 64, 1000], P(None, 'dp', 'section')
- variance: float32 [2, 64, 1000], P(None, 'dp', 'section')
All inputs are finite; a program needn't handle non-finite values.
Results may differ from a plain program's by a relative error of at most 0.018.
Values may be sent and summed in bfloat16 or wider, within the bound.
No kernel may reach another device: no remote copies, remote signals or barrier semaphores. Data moves between devices by JAX's collectives and lax.ppermute only.
A program may use at most 64 MiB of HBM per device.

v0:
```python
import jax
import jax.numpy as jnp
from jax import lax
from jax.sharding import PartitionSpec as P

HEADS = 8
HEAD = 64
TANGENTS = 2
HD = 512
epsilon = 1e-06


def gather_turned(arrays, axis, dims):
    turned = [jnp.moveaxis(a, dim, 0) for a, dim in zip(arrays, dims)]
    both = jnp.concatenate([t.reshape(len(t), -1) for t in turned], axis=1)
    result, at, gathered = (lax.all_gather(both, axis, axis=0, tiled=True), 0, [])
    for t, dim in zip(turned, dims):
        share = result[:, at : at + t[0].size].reshape(-1, *t.shape[1:])
        gathered.append(jnp.moveaxis(share, 0, dim))
        at += t[0].size
    return tuple(gathered)


def passed_along(block, axis, distance):
    devices = range(lax.axis_size(axis))
    route = [(i - distance, i) for i in devices if i - distance in devices]
    return lax.ppermute(block, axis, route)


def picked(shard, axis, root):
    return lax.dynamic_index_in_dim(lax.all_gather(shard, axis), root, 0, keepdims=False)


def contract(spec, left, right):
    return jnp.einsum(spec, left, right, preferred_element_type=jnp.float32)


def norm_jvp(primal, tangents, gains):
    average = jnp.mean(primal, -1, keepdims=True)
    centred = primal - average
    inverse = lax.rsqrt(jnp.mean(centred * centred, -1, keepdims=True) + epsilon)
    dcentred = tangents - jnp.mean(tangents, -1, keepdims=True)
    dinverse = -(inverse**3) * jnp.mean(centred * dcentred, -1, keepdims=True)
    return (centred * inverse * gains, (dcentred * inverse + centred * dinverse) * gains)


def layer_step(state, qkv_weight, out_weight, value_tangent, out_tangent, gains):
    resid = state.astype(jnp.float32)
    normed_zero, normed_rest = norm_jvp(resid[0], resid[1:], gains)
    normed = jnp.concatenate([normed_zero[None], normed_rest]).astype(jnp.bfloat16)
    streams, batch, tokens_here, width = normed.shape
    projected = contract("sbtd,de->sbte", normed, qkv_weight)
    extra_value = contract("btd,kde->kbte", normed[0], value_tangent)
    queries = projected[..., :HD]
    key_rows = projected[..., HD : 2 * HD]
    values = projected[..., 2 * HD :]
    values = jnp.concatenate([values[:1], values[1:] + extra_value])
    shape_heads = (streams, batch, tokens_here, HEADS, HEAD)
    queries = queries.astype(jnp.bfloat16).reshape(shape_heads)
    key_rows = key_rows.astype(jnp.bfloat16).reshape(shape_heads)
    values = values.astype(jnp.bfloat16).reshape(shape_heads)
    factor = HEAD ** (-0.5)
    scores = contract("bqhe,bkhe->bhqk", queries[0], key_rows[0]) * factor
    probs = jax.nn.softmax(scores, -1)
    dscores = (
        contract("sbqhe,bkhe->sbhqk", queries[1:], key_rows[0])
        + contract("bqhe,sbkhe->sbhqk", queries[0], key_rows[1:])
    ) * factor
    dprobs = probs * (dscores - jnp.sum(probs * dscores, -1, keepdims=True))
    probs_low = probs.astype(jnp.bfloat16)
    dprobs_low = dprobs.astype(jnp.bfloat16)
    attended_zero = contract("bhqk,bkhe->bqhe", probs_low, values[0])
    attended_rest = contract("sbhqk,bkhe->sbqhe", dprobs_low, values[0]) + contract(
        "bhqk,sbkhe->sbqhe", probs_low, values[1:]
    )
    attended = jnp.concatenate([attended_zero[None], attended_rest]).astype(jnp.bfloat16)
    attended = attended.reshape(streams, batch, tokens_here, HD)
    output = contract("sbte,ed->sbtd", attended, out_weight)
    extra_out = contract("bte,ked->kbtd", attended[0], out_tangent)
    output = jnp.concatenate([output[:1], output[1:] + extra_out])
    return (resid + output).astype(jnp.bfloat16)


def shards(tokens, w_qkv, w_output, tangent_value, tangent_output, layer_gain, final_gain, head):
    full_qkv, full_output, full_value_tan, full_output_tan = gather_turned(
        (w_qkv, w_output, tangent_value, tangent_output), "dp", (1, 2, 2, 3)
    )
    section_gain = layer_gain[0]

    def advance_layer(state):
        return layer_step(
            state, full_qkv[0], full_output[0], full_value_tan[0], full_output_tan[0], section_gain
        )

    def blank_layer(state):
        return jnp.zeros_like(state)

    section_index = lax.axis_index("section")
    section_count = lax.axis_size("section")
    micro_count = tokens.shape[0]
    image_tokens = tokens.shape[2]
    model_width = tokens.shape[3]
    streams = TANGENTS + 1
    flat_tokens = tokens.reshape(micro_count, image_tokens, model_width)

    def advance(step, carried):
        outgoing, collected = carried
        incoming = passed_along(outgoing, "section", 1)
        source_pick = jnp.clip(step, 0, micro_count - 1)
        source_rows = lax.dynamic_index_in_dim(flat_tokens, source_pick, 0, keepdims=True)
        entering = jnp.concatenate(
            [source_rows[None], jnp.zeros((TANGENTS, 1, image_tokens, model_width), jnp.bfloat16)]
        )
        source = jnp.where(section_index == 0, entering, incoming)
        micro_slot = step - section_index
        active = (micro_slot >= 0) & (micro_slot < micro_count)
        result = lax.cond(active, advance_layer, blank_layer, source)
        store_here = active & (section_index == section_count - 1)
        slot_clip = jnp.clip(micro_slot, 0, micro_count - 1)
        current = lax.dynamic_index_in_dim(collected, slot_clip, 1, keepdims=True)
        update = jnp.where(store_here, result[:, :, 0, :], current)
        collected = lax.dynamic_update_slice_in_dim(collected, update, slot_clip, 1)
        return (result, collected)

    initial = (
        jnp.zeros((streams, 1, image_tokens, model_width), jnp.bfloat16),
        jnp.zeros((streams, micro_count, model_width), jnp.bfloat16),
    )
    ignored, collected = lax.fori_loop(0, section_count + micro_count - 1, advance, initial)
    features = picked(collected, "section", section_count - 1)
    widened = features.astype(jnp.float32)
    final_zero, final_rest = norm_jvp(widened[0], widened[1:], final_gain)
    normed_final = jnp.concatenate([final_zero[None], final_rest]).astype(jnp.bfloat16)
    logits = contract("sbd,dc->sbc", normed_final, head)
    mean_logits = logits[0][:, None, :]
    variance = jnp.sum(logits[1:] * logits[1:], 0)[:, None, :]
    return (mean_logits, variance)


def solution(mesh):
    return jax.shard_map(
        shards,
        mesh=mesh,
        in_specs=(
            P(None, "dp", None, None),
            P("section", "dp", None),
            P("section", None, "dp"),
            P("section", None, "dp", None),
            P("section", None, None, "dp"),
            P("section", None),
            P(),
            P(None, "section"),
        ),
        out_specs=(P(None, "dp", "section"), P(None, "dp", "section")),
        check_vma=False,
    )
```

profile of v0, /device:TPU:5, one launch (start us, length us, event | category | flops | bytes accessed | tf_op | source)
XLA Modules:
  0.0 661.8 jit_solution(5009150919877096323)
XLA Ops:
  8.9 1.5 pad_maximum_fusion
  10.4 271.7 %all-gather.3.cloned.1.call-done = bf16[1024,4096]{1,0:T(8,128)(2,1)} async-done(((bf16[16,4096]{1,0:T(8,128)(2,1)}), bf16[1024,4096]{1,0:T(8,128)(2,1)}) %all-gather.3.cloned.1.call-update) | async-done | bytes 8388624 | tf_op jit(solution)/shard_map/all_gather | solution.py:16
  282.1 4.6 fusion.96
  286.8 3.3 reshape.530
  290.1 1.8 copy.141
  291.8 4.0 copy.92
  295.8 1.3 slice_bitcast_fusion.2
  297.1 1.3 copy.72
  298.4 3.9 slice.162
  303.7 272.0 %while.16 = (s32[]{:T(128)}, bf16[3,1,80,1024]{3,2,0,1:T(8,128)(2,1)}, bf16[3,2,1024]{2,0,1:T(4,128)(2,1)}, s32[]{:T(128)}, pred[]{:T(512)}, /*index=5*/bf16[2,8...) while((s32[]{:T(128)}, ...), condition=%wide.region_10.11_spmd, body=%wide.region_0.10_spmd.sunk | while | flops 1414402304 | bytes 55991232 | solution.py:129
  303.7 47.9 %collective-permute-start = (bf16[3,1,80,1024]{3,2,0,1:T(8,128)(2,1)}, bf16[3,1,80,1024]{3,2,0,1:T(8,128)(2,1)S(1)}, u32[]{:S(2)}, u32[]{:S(2)}) collective-permute-start(bf16[3,1,80,1024]{3,2,0,1:T(8,128)(2,1)} %get-tuple-element.501), channel_id=1, source_target_pairs={{0,64},{64,128},{128,192},{192,256},{256,320},{320,384},{384,448},... | collective-permute-start | bytes 1474568 | tf_op jit(solution)/shard_map/while/body/eval_jaxpr/ppermute | solution.py:27
  351.6 6.0 collective-permute-done
  357.7 1.4 conditional.2
  359.1 1.3 select_dynamic-update-slice_fusion.2
  360.4 5.2 collective-permute-start
  365.6 12.1 %collective-permute-done = bf16[3,1,80,1024]{3,2,0,1:T(8,128)(2,1)S(1)} collective-permute-done((bf16[3,1,80,1024]{3,2,0,1:T(8,128)(2,1)}, bf16[3,1,80,1024]{3,2,0,1:T(8,128)(2,1)S(1)}, u32[]{:S(2)}, u32[]{:S(2)}) %collective-permute-start) | collective-permute-done | bytes 491552 | tf_op jit(solution)/shard_map/while/body/eval_jaxpr/ppermute | solution.py:27
  377.7 23.2 %conditional.2 = (bf16[3,1,80,1024]{3,2,0,1:T(8,128)(2,1)}, bf16[3,1,1024]{2,0,1:T(4,128)(2,1)}) conditional(s32[]{:T(128)} %convert_element_type.96, () %tuple.75, (pred[]{:T(512)}, s32[]{:T(128)}, bf16[2,80,1024]{2,1,0:T(8,128)(2,1)}, bf16[3,1,80,1024]{3,2,0,1:T(8,128)(2,1)S(1)}, f32[1,1024]{1,0:T(1,128)S(1)}, ...), branch_computations={%region_1.1_spmd, %region_2.9_spmd} | conditional | flops 1414399232 | bytes 54000248 | solution.py:117
  379.7 0.9 copy-done.1
  380.7 2.1 fusion.90
  384.5 1.2 convolution_bitcast_fusion
  385.9 1.0 fusion.91
  386.9 1.8 broadcast_multiply_fusion
  389.6 1.7 multiply_reduce_fusion
  391.5 1.5 fusion.27
  394.7 1.6 fusion.30
  396.4 2.1 fusion.14
  400.9 1.3 select_dynamic-update-slice_fusion.2
  402.2 1.9 collective-permute-start
  404.1 6.0 collective-permute-done
  410.1 23.2 %conditional.2 = (bf16[3,1,80,1024]{3,2,0,1:T(8,128)(2,1)}, bf16[3,1,1024]{2,0,1:T(4,128)(2,1)}) conditional(s32[]{:T(128)} %convert_element_type.96, () %tuple.75, (pred[]{:T(512)}, s32[]{:T(128)}, bf16[2,80,1024]{2,1,0:T(8,128)(2,1)}, bf16[3,1,80,1024]{3,2,0,1:T(8,128)(2,1)S(1)}, f32[1,1024]{1,0:T(1,128)S(1)}, ...), branch_computations={%region_1.1_spmd, %region_2.9_spmd} | conditional | flops 1414399232 | bytes 54000248 | solution.py:117
  413.2 2.1 fusion.90
  417.0 1.2 convolution_bitcast_fusion
  418.4 1.0 fusion.91
  419.4 1.8 broadcast_multiply_fusion
  422.1 1.7 multiply_reduce_fusion
  424.0 1.5 fusion.27
  427.2 1.6 fusion.30
  428.9 2.1 fusion.14
  433.4 1.3 select_dynamic-update-slice_fusion.2
  434.7 5.2 collective-permute-start
  439.9 6.0 collective-permute-done
  445.9 1.4 conditional.2
  447.3 1.3 select_dynamic-update-slice_fusion.2
  448.6 27.0 %collective-permute-start = (bf16[3,1,80,1024]{3,2,0,1:T(8,128)(2,1)}, bf16[3,1,80,1024]{3,2,0,1:T(8,128)(2,1)S(1)}, u32[]{:S(2)}, u32[]{:S(2)}) collective-permute-start(bf16[3,1,80,1024]{3,2,0,1:T(8,128)(2,1)} %get-tuple-element.501), channel_id=1, source_target_pairs={{0,64},{64,128},{128,192},{192,256},{256,320},{320,384},{384,448},... | collective-permute-start | bytes 1474568 | tf_op jit(solution)/shard_map/while/body/eval_jaxpr/ppermute | solution.py:27
  475.6 6.1 collective-permute-done
  481.7 1.4 conditional.2
  483.1 1.3 select_dynamic-update-slice_fusion.2
  484.4 5.2 collective-permute-start
  489.7 6.0 collective-permute-done
  495.7 1.4 conditional.2
  497.2 1.3 select_dynamic-update-slice_fusion.2
  498.5 13.9 %collective-permute-start = (bf16[3,1,80,1024]{3,2,0,1:T(8,128)(2,1)}, bf16[3,1,80,1024]{3,2,0,1:T(8,128)(2,1)S(1)}, u32[]{:S(2)}, u32[]{:S(2)}) collective-permute-start(bf16[3,1,80,1024]{3,2,0,1:T(8,128)(2,1)} %get-tuple-element.501), channel_id=1, source_target_pairs={{0,64},{64,128},{128,192},{192,256},{256,320},{320,384},{384,448},... | collective-permute-start | bytes 1474568 | tf_op jit(solution)/shard_map/while/body/eval_jaxpr/ppermute | solution.py:27
  512.4 6.0 collective-permute-done
  518.4 1.4 conditional.2
  519.9 1.3 select_dynamic-update-slice_fusion.2
  521.2 8.7 %collective-permute-start = (bf16[3,1,80,1024]{3,2,0,1:T(8,128)(2,1)}, bf16[3,1,80,1024]{3,2,0,1:T(8,128)(2,1)S(1)}, u32[]{:S(2)}, u32[]{:S(2)}) collective-permute-start(bf16[3,1,80,1024]{3,2,0,1:T(8,128)(2,1)} %get-tuple-element.501), channel_id=1, source_target_pairs={{0,64},{64,128},{128,192},{192,256},{256,320},{320,384},{384,448},... | collective-permute-start | bytes 1474568 | tf_op jit(solution)/shard_map/while/body/eval_jaxpr/ppermute | solution.py:27
  529.9 6.0 collective-permute-done
  536.0 1.4 conditional.2
  537.4 1.3 select_dynamic-update-slice_fusion.2
  538.7 28.2 %collective-permute-start = (bf16[3,1,80,1024]{3,2,0,1:T(8,128)(2,1)}, bf16[3,1,80,1024]{3,2,0,1:T(8,128)(2,1)S(1)}, u32[]{:S(2)}, u32[]{:S(2)}) collective-permute-start(bf16[3,1,80,1024]{3,2,0,1:T(8,128)(2,1)} %get-tuple-element.501), channel_id=1, source_target_pairs={{0,64},{64,128},{128,192},{192,256},{256,320},{320,384},{384,448},... | collective-permute-start | bytes 1474568 | tf_op jit(solution)/shard_map/while/body/eval_jaxpr/ppermute | solution.py:27
  567.0 6.0 collective-permute-done
  573.0 1.4 conditional.2
  574.4 1.3 select_dynamic-update-slice_fusion.2
  576.5 74.9 %all-gather = bf16[24,2,1024]{2,1,0:T(2,128)(2,1)S(1)} all-gather(bf16[3,2,1024]{2,1,0:T(2,128)(2,1)S(1)} %copy.73), channel_id=2, replica_groups=mesh['section'=8,'dp'=64] {'section'}, dimensions={0}, use_global_device_ids=true | all-gather | bytes 110592 | tf_op jit(solution)/shard_map/all_gather | solution.py:31
  (122 shorter events, 36.4 us)
Async XLA Ops:
  7.2 646.4 %copy-start = (bf16[1024,125]{1,0:T(8,128)(2,1)S(1)}, bf16[1024,125]{1,0:T(8,128)(2,1)}, u32[]{:S(2)}) copy-start(bf16[1024,125]{1,0:T(8,128)(2,1)} %param.19) | copy-start | bytes 768004
  7.2 274.9 %all-gather.3.cloned.1.call-start = ((), (), s32[]{:S(2)}) async-start(), calls=%async_computation | async-start | bytes 8519680 | tf_op jit(solution)/shard_map/all_gather | solution.py:16
  298.4 5.3 copy-start.5
  303.7 54.0 %collective-permute-start = (bf16[3,1,80,1024]{3,2,0,1:T(8,128)(2,1)}, bf16[3,1,80,1024]{3,2,0,1:T(8,128)(2,1)S(1)}, u32[]{:S(2)}, u32[]{:S(2)}) collective-permute-start(bf16[3,1,80,1024]{3,2,0,1:T(8,128)(2,1)} %get-tuple-element.501), channel_id=1, source_target_pairs={{0,64},{64,128},{128,192},{192,256},{256,320},{320,384},{384,448},... | collective-permute-start | bytes 1474568 | tf_op jit(solution)/shard_map/while/body/eval_jaxpr/ppermute | solution.py:27
  360.4 17.2 %collective-permute-start = (bf16[3,1,80,1024]{3,2,0,1:T(8,128)(2,1)}, bf16[3,1,80,1024]{3,2,0,1:T(8,128)(2,1)S(1)}, u32[]{:S(2)}, u32[]{:S(2)}) collective-permute-start(bf16[3,1,80,1024]{3,2,0,1:T(8,128)(2,1)} %get-tuple-element.501), channel_id=1, source_target_pairs={{0,64},{64,128},{128,192},{192,256},{256,320},{320,384},{384,448},... | collective-permute-start | bytes 1474568 | tf_op jit(solution)/shard_map/while/body/eval_jaxpr/ppermute | solution.py:27
  378.8 1.9 copy-start.1
  379.0 3.8 copy-start.6
  385.9 3.7 copy-start.3
  389.6 1.9 copy-start.2
  391.5 2.0 copy-start.4
  402.2 8.0 %collective-permute-start = (bf16[3,1,80,1024]{3,2,0,1:T(8,128)(2,1)}, bf16[3,1,80,1024]{3,2,0,1:T(8,128)(2,1)S(1)}, u32[]{:S(2)}, u32[]{:S(2)}) collective-permute-start(bf16[3,1,80,1024]{3,2,0,1:T(8,128)(2,1)} %get-tuple-element.501), channel_id=1, source_target_pairs={{0,64},{64,128},{128,192},{192,256},{256,320},{320,384},{384,448},... | collective-permute-start | bytes 1474568 | tf_op jit(solution)/shard_map/while/body/eval_jaxpr/ppermute | solution.py:27
  411.3 1.9 copy-start.1
  411.5 3.8 copy-start.6
  418.4 3.7 copy-start.3
  422.1 1.9 copy-start.2
  424.0 2.0 copy-start.4
  434.7 11.2 %collective-permute-start = (bf16[3,1,80,1024]{3,2,0,1:T(8,128)(2,1)}, bf16[3,1,80,1024]{3,2,0,1:T(8,128)(2,1)S(1)}, u32[]{:S(2)}, u32[]{:S(2)}) collective-permute-start(bf16[3,1,80,1024]{3,2,0,1:T(8,128)(2,1)} %get-tuple-element.501), channel_id=1, source_target_pairs={{0,64},{64,128},{128,192},{192,256},{256,320},{320,384},{384,448},... | collective-permute-start | bytes 1474568 | tf_op jit(solution)/shard_map/while/body/eval_jaxpr/ppermute | solution.py:27
  448.6 33.1 %collective-permute-start = (bf16[3,1,80,1024]{3,2,0,1:T(8,128)(2,1)}, bf16[3,1,80,1024]{3,2,0,1:T(8,128)(2,1)S(1)}, u32[]{:S(2)}, u32[]{:S(2)}) collective-permute-start(bf16[3,1,80,1024]{3,2,0,1:T(8,128)(2,1)} %get-tuple-element.501), channel_id=1, source_target_pairs={{0,64},{64,128},{128,192},{192,256},{256,320},{320,384},{384,448},... | collective-permute-start | bytes 1474568 | tf_op jit(solution)/shard_map/while/body/eval_jaxpr/ppermute | solution.py:27
  484.4 11.3 %collective-permute-start = (bf16[3,1,80,1024]{3,2,0,1:T(8,128)(2,1)}, bf16[3,1,80,1024]{3,2,0,1:T(8,128)(2,1)S(1)}, u32[]{:S(2)}, u32[]{:S(2)}) collective-permute-start(bf16[3,1,80,1024]{3,2,0,1:T(8,128)(2,1)} %get-tuple-element.501), channel_id=1, source_target_pairs={{0,64},{64,128},{128,192},{192,256},{256,320},{320,384},{384,448},... | collective-permute-start | bytes 1474568 | tf_op jit(solution)/shard_map/while/body/eval_jaxpr/ppermute | solution.py:27
  498.5 20.0 %collective-permute-start = (bf16[3,1,80,1024]{3,2,0,1:T(8,128)(2,1)}, bf16[3,1,80,1024]{3,2,0,1:T(8,128)(2,1)S(1)}, u32[]{:S(2)}, u32[]{:S(2)}) collective-permute-start(bf16[3,1,80,1024]{3,2,0,1:T(8,128)(2,1)} %get-tuple-element.501), channel_id=1, source_target_pairs={{0,64},{64,128},{128,192},{192,256},{256,320},{320,384},{384,448},... | collective-permute-start | bytes 1474568 | tf_op jit(solution)/shard_map/while/body/eval_jaxpr/ppermute | solution.py:27
  521.2 14.8 %collective-permute-start = (bf16[3,1,80,1024]{3,2,0,1:T(8,128)(2,1)}, bf16[3,1,80,1024]{3,2,0,1:T(8,128)(2,1)S(1)}, u32[]{:S(2)}, u32[]{:S(2)}) collective-permute-start(bf16[3,1,80,1024]{3,2,0,1:T(8,128)(2,1)} %get-tuple-element.501), channel_id=1, source_target_pairs={{0,64},{64,128},{128,192},{192,256},{256,320},{320,384},{384,448},... | collective-permute-start | bytes 1474568 | tf_op jit(solution)/shard_map/while/body/eval_jaxpr/ppermute | solution.py:27
  538.7 34.3 %collective-permute-start = (bf16[3,1,80,1024]{3,2,0,1:T(8,128)(2,1)}, bf16[3,1,80,1024]{3,2,0,1:T(8,128)(2,1)S(1)}, u32[]{:S(2)}, u32[]{:S(2)}) collective-permute-start(bf16[3,1,80,1024]{3,2,0,1:T(8,128)(2,1)} %get-tuple-element.501), channel_id=1, source_target_pairs={{0,64},{64,128},{128,192},{192,256},{256,320},{320,384},{384,448},... | collective-permute-start | bytes 1474568 | tf_op jit(solution)/shard_map/while/body/eval_jaxpr/ppermute | solution.py:27
Sparse Core Ops, SparseCore 0:
  10.5 271.5 all-gather.2
where the time goes:
time: 664 us; the launch traced here: 662 us
  waiting for transfers between devices  332 us (50%)
  starting transfers between devices  143 us (22%)
  blocking collectives  74.9 us (11%)
  local copies, waits for them, and re-layouts  48.8 us (7%)
  matrix products  24.3 us (4%)
  other arithmetic  23.5 us (4%)
  between operations  14.1 us (2%)
    all_gather x1, waiting for transfers between devices, gather_turned(): lax.all_gather(both, axis, axis=0, tiled=True)  272 us
    ppermute x9, starting transfers between devices, passed_along(): return lax.ppermute(block, axis, route)  143 us
    all_gather x1, blocking collectives, picked(): lax.all_gather(shard, axis)  74.9 us
    ppermute x9, waiting for transfers between devices, passed_along(): return lax.ppermute(block, axis, route)  60.5 us
    dot_general x19, matrix products, contract(): return jnp.einsum(spec, left, right, preferred_element_type=jnp.float32)  22.4 us
  transfers between devices with their start and end apart: 10, of which 10 were waited for; matrix products, arithmetic and copies ran while one was open for 0% of the time, Pallas kernels for 0%

commit v1 on v0

--- a/solution.py
+++ b/solution.py
@@ -10,10 +10,17 @@
 epsilon = 1e-06
 
 
+def all_by_exchange(x, axis, dim):
+    size = lax.axis_size(axis)
+    blocks = jnp.stack([x for _ in range(size)])
+    blocks = lax.all_to_all(blocks, axis, split_axis=0, concat_axis=0)
+    return jnp.concatenate(blocks, axis=dim)
+
+
 def gather_turned(arrays, axis, dims):
     turned = [jnp.moveaxis(a, dim, 0) for a, dim in zip(arrays, dims)]
     both = jnp.concatenate([t.reshape(len(t), -1) for t in turned], axis=1)
-    result, at, gathered = (lax.all_gather(both, axis, axis=0, tiled=True), 0, [])
+    result, at, gathered = (all_by_exchange(both, axis, 0), 0, [])
     for t, dim in zip(turned, dims):
         share = result[:, at : at + t[0].size].reshape(-1, *t.shape[1:])
         gathered.append(jnp.moveaxis(share, 0, dim))

time: 664 us -> 533 us (0.80)
  the two profiles are of different devices: /device:TPU:5 before, /device:TPU:69 now
where the time goes in v1:
time: 533 us; the launch traced here: 531 us
  waiting for transfers between devices  247 us (46%)
  starting transfers between devices  109 us (20%)
  blocking collectives  73.5 us (14%)
  local copies, waits for them, and re-layouts  53.1 us (10%)
  matrix products  24.4 us (5%)
  other arithmetic  22.9 us (4%)
    all_to_all x1, waiting for transfers between devices, all_by_exchange(): blocks = lax.all_to_all(blocks, axis, split_axis=0, concat_axis=0)  183 us
    ppermute x9, starting transfers between devices, passed_along(): return lax.ppermute(block, axis, route)  97.6 us
    all_gather x1, blocking collectives, picked(): lax.all_gather(shard, axis)  73.5 us
    ppermute x9, waiting for transfers between devices, passed_along(): return lax.ppermute(block, axis, route)  64.3 us
    dot_general x19, matrix products, contract(): return jnp.einsum(spec, left, right, preferred_element_type=jnp.float32)  22.4 us
    another operation x22, local copies, waits for them, and re-layouts  12.1 us
    dynamic_update_slice x9, other arithmetic, advance(): collected = lax.dynamic_update_slice_in_dim(collected, update, slot_clip, 1)  11.7 us
    all_to_all x1, starting transfers between devices, all_by_exchange(): blocks = lax.all_to_all(blocks, axis, split_axis=0, concat_axis=0)  11.2 us
  transfers between devices with their start and end apart: 10, of which 10 were waited for; matrix products, arithmetic and copies ran while one was open for 0% of the time, Pallas kernels for 0%

profile of v1, /device:TPU:69, one launch (start us, length us, event | category | flops | bytes accessed | tf_op | source)
XLA Modules:
  0.0 530.9 jit_solution(3454206021531455515)
XLA Ops:
  3.1 4.3 stack.2
  7.4 11.2 %all-to-all-start = ((bf16[64,16,4096]{2,1,0:T(8,128)(2,1)}), bf16[64,16,4096]{2,1,0:T(8,128)(2,1)}, u32[]{:S(2)}, u32[]{:S(2)}) async-start(bf16[64,16,4096]{2,1,0:T(8,128)(2,1)} %stack.2), calls=%async_computation | async-start | bytes 16777216 | tf_op jit(solution)/shard_map/all_to_all | solution.py:16
  18.6 182.6 %all-to-all-done = bf16[64,16,4096]{2,1,0:T(8,128)(2,1)} async-done(((bf16[64,16,4096]{2,1,0:T(8,128)(2,1)}), bf16[64,16,4096]{2,1,0:T(8,128)(2,1)}, u32[]{:S(2)}, u32[]{:S(2)}) %all-to-all-start) | async-done | bytes 8388640 | tf_op jit(solution)/shard_map/all_to_all | solution.py:16
  201.2 4.7 fusion.96
  205.9 3.8 slice.162
  209.7 1.3 slice_bitcast_fusion.2
  211.0 3.3 reshape.536
  214.3 1.7 copy.137
  216.0 4.0 copy.88
  220.0 1.3 copy.68
  222.7 230.4 %while.16 = (s32[]{:T(128)}, bf16[3,1,80,1024]{3,2,0,1:T(8,128)(2,1)}, bf16[3,2,1024]{2,0,1:T(4,128)(2,1)}, s32[]{:T(128)}, pred[]{:T(512)}, /*index=5*/bf16[2,8...) while((s32[]{:T(128)}, ...), condition=%wide.region_10.11_spmd, body=%wide.region_0.10_spmd.sunk | while | flops 1414402304 | bytes 55991232 | solution.py:136
  222.7 9.7 %collective-permute-start = (bf16[3,1,80,1024]{3,2,0,1:T(8,128)(2,1)}, bf16[3,1,80,1024]{3,2,0,1:T(8,128)(2,1)S(1)}, u32[]{:S(2)}, u32[]{:S(2)}) collective-permute-start(bf16[3,1,80,1024]{3,2,0,1:T(8,128)(2,1)} %get-tuple-element.501), channel_id=1, source_target_pairs={{0,64},{64,128},{128,192},{192,256},{256,320},{320,384},{384,448},... | collective-permute-start | bytes 1474568 | tf_op jit(solution)/shard_map/while/body/eval_jaxpr/ppermute | solution.py:34
  232.5 11.3 %collective-permute-done = bf16[3,1,80,1024]{3,2,0,1:T(8,128)(2,1)S(1)} collective-permute-done((bf16[3,1,80,1024]{3,2,0,1:T(8,128)(2,1)}, bf16[3,1,80,1024]{3,2,0,1:T(8,128)(2,1)S(1)}, u32[]{:S(2)}, u32[]{:S(2)}) %collective-permute-start) | collective-permute-done | bytes 491552 | tf_op jit(solution)/shard_map/while/body/eval_jaxpr/ppermute | solution.py:34
  243.8 1.4 conditional.2
  245.3 1.3 select_dynamic-update-slice_fusion.2
  246.5 5.2 collective-permute-start
  251.8 6.1 %collective-permute-done = bf16[3,1,80,1024]{3,2,0,1:T(8,128)(2,1)S(1)} collective-permute-done((bf16[3,1,80,1024]{3,2,0,1:T(8,128)(2,1)}, bf16[3,1,80,1024]{3,2,0,1:T(8,128)(2,1)S(1)}, u32[]{:S(2)}, u32[]{:S(2)}) %collective-permute-start) | collective-permute-done | bytes 491552 | tf_op jit(solution)/shard_map/while/body/eval_jaxpr/ppermute | solution.py:34
  257.9 23.3 %conditional.2 = (bf16[3,1,80,1024]{3,2,0,1:T(8,128)(2,1)}, bf16[3,1,1024]{2,0,1:T(4,128)(2,1)}) conditional(s32[]{:T(128)} %convert_element_type.96, () %tuple.75, (pred[]{:T(512)}, s32[]{:T(128)}, bf16[2,80,1024]{2,1,0:T(8,128)(2,1)}, bf16[3,1,80,1024]{3,2,0,1:T(8,128)(2,1)S(1)}, f32[1,1024]{1,0:T(1,128)S(1)}, ...), branch_computations={%region_1.1_spmd, %region_2.9_spmd} | conditional | flops 1414399232 | bytes 54000248 | solution.py:124
  260.9 2.1 fusion.90
  264.8 1.2 convolution_bitcast_fusion
  266.1 1.0 fusion.91
  267.2 1.7 broadcast_multiply_fusion
  269.9 1.7 multiply_reduce_fusion
  271.7 1.5 fusion.27
  275.0 1.6 fusion.30
  276.7 2.1 fusion.14
  281.1 1.3 select_dynamic-update-slice_fusion.2
  282.4 1.9 collective-permute-start
  284.4 10.6 %collective-permute-done = bf16[3,1,80,1024]{3,2,0,1:T(8,128)(2,1)S(1)} collective-permute-done((bf16[3,1,80,1024]{3,2,0,1:T(8,128)(2,1)}, bf16[3,1,80,1024]{3,2,0,1:T(8,128)(2,1)S(1)}, u32[]{:S(2)}, u32[]{:S(2)}) %collective-permute-start) | collective-permute-done | bytes 491552 | tf_op jit(solution)/shard_map/while/body/eval_jaxpr/ppermute | solution.py:34
  294.9 23.2 %conditional.2 = (bf16[3,1,80,1024]{3,2,0,1:T(8,128)(2,1)}, bf16[3,1,1024]{2,0,1:T(4,128)(2,1)}) conditional(s32[]{:T(128)} %convert_element_type.96, () %tuple.75, (pred[]{:T(512)}, s32[]{:T(128)}, bf16[2,80,1024]{2,1,0:T(8,128)(2,1)}, bf16[3,1,80,1024]{3,2,0,1:T(8,128)(2,1)S(1)}, f32[1,1024]{1,0:T(1,128)S(1)}, ...), branch_computations={%region_1.1_spmd, %region_2.9_spmd} | conditional | flops 1414399232 | bytes 54000248 | solution.py:124
  298.0 2.1 fusion.90
  301.8 1.2 convolution_bitcast_fusion
  303.2 1.0 fusion.91
  304.2 1.7 broadcast_multiply_fusion
  306.9 1.7 multiply_reduce_fusion
  308.8 1.5 fusion.27
  312.1 1.6 fusion.30
  313.7 2.1 fusion.14
  318.2 1.3 select_dynamic-update-slice_fusion.2
  319.5 5.2 collective-permute-start
  324.7 6.0 %collective-permute-done = bf16[3,1,80,1024]{3,2,0,1:T(8,128)(2,1)S(1)} collective-permute-done((bf16[3,1,80,1024]{3,2,0,1:T(8,128)(2,1)}, bf16[3,1,80,1024]{3,2,0,1:T(8,128)(2,1)S(1)}, u32[]{:S(2)}, u32[]{:S(2)}) %collective-permute-start) | collective-permute-done | bytes 491552 | tf_op jit(solution)/shard_map/while/body/eval_jaxpr/ppermute | solution.py:34
  330.8 1.4 conditional.2
  332.2 1.3 select_dynamic-update-slice_fusion.2
  333.5 27.0 %collective-permute-start = (bf16[3,1,80,1024]{3,2,0,1:T(8,128)(2,1)}, bf16[3,1,80,1024]{3,2,0,1:T(8,128)(2,1)S(1)}, u32[]{:S(2)}, u32[]{:S(2)}) collective-permute-start(bf16[3,1,80,1024]{3,2,0,1:T(8,128)(2,1)} %get-tuple-element.501), channel_id=1, source_target_pairs={{0,64},{64,128},{128,192},{192,256},{256,320},{320,384},{384,448},... | collective-permute-start | bytes 1474568 | tf_op jit(solution)/shard_map/while/body/eval_jaxpr/ppermute | solution.py:34
  360.5 6.0 %collective-permute-done = bf16[3,1,80,1024]{3,2,0,1:T(8,128)(2,1)S(1)} collective-permute-done((bf16[3,1,80,1024]{3,2,0,1:T(8,128)(2,1)}, bf16[3,1,80,1024]{3,2,0,1:T(8,128)(2,1)S(1)}, u32[]{:S(2)}, u32[]{:S(2)}) %collective-permute-start) | collective-permute-done | bytes 491552 | tf_op jit(solution)/shard_map/while/body/eval_jaxpr/ppermute | solution.py:34
  366.6 1.4 conditional.2
  368.0 1.3 select_dynamic-update-slice_fusion.2
  369.3 5.2 collective-permute-start
  374.5 6.0 %collective-permute-done = bf16[3,1,80,1024]{3,2,0,1:T(8,128)(2,1)S(1)} collective-permute-done((bf16[3,1,80,1024]{3,2,0,1:T(8,128)(2,1)}, bf16[3,1,80,1024]{3,2,0,1:T(8,128)(2,1)S(1)}, u32[]{:S(2)}, u32[]{:S(2)}) %collective-permute-start) | collective-permute-done | bytes 491552 | tf_op jit(solution)/shard_map/while/body/eval_jaxpr/ppermute | solution.py:34
  380.6 1.4 conditional.2
  382.0 1.3 select_dynamic-update-slice_fusion.2
  383.3 12.0 %collective-permute-start = (bf16[3,1,80,1024]{3,2,0,1:T(8,128)(2,1)}, bf16[3,1,80,1024]{3,2,0,1:T(8,128)(2,1)S(1)}, u32[]{:S(2)}, u32[]{:S(2)}) collective-permute-start(bf16[3,1,80,1024]{3,2,0,1:T(8,128)(2,1)} %get-tuple-element.501), channel_id=1, source_target_pairs={{0,64},{64,128},{128,192},{192,256},{256,320},{320,384},{384,448},... | collective-permute-start | bytes 1474568 | tf_op jit(solution)/shard_map/while/body/eval_jaxpr/ppermute | solution.py:34
  395.4 6.0 %collective-permute-done = bf16[3,1,80,1024]{3,2,0,1:T(8,128)(2,1)S(1)} collective-permute-done((bf16[3,1,80,1024]{3,2,0,1:T(8,128)(2,1)}, bf16[3,1,80,1024]{3,2,0,1:T(8,128)(2,1)S(1)}, u32[]{:S(2)}, u32[]{:S(2)}) %collective-permute-start) | collective-permute-done | bytes 491552 | tf_op jit(solution)/shard_map/while/body/eval_jaxpr/ppermute | solution.py:34
  401.4 1.4 conditional.2
  402.9 1.3 select_dynamic-update-slice_fusion.2
  404.2 5.2 collective-permute-start
  409.4 6.0 %collective-permute-done = bf16[3,1,80,1024]{3,2,0,1:T(8,128)(2,1)S(1)} collective-permute-done((bf16[3,1,80,1024]{3,2,0,1:T(8,128)(2,1)}, bf16[3,1,80,1024]{3,2,0,1:T(8,128)(2,1)S(1)}, u32[]{:S(2)}, u32[]{:S(2)}) %collective-permute-start) | collective-permute-done | bytes 491552 | tf_op jit(solution)/shard_map/while/body/eval_jaxpr/ppermute | solution.py:34
  415.4 1.4 conditional.2
  416.8 1.3 select_dynamic-update-slice_fusion.2
  418.1 26.1 %collective-permute-start = (bf16[3,1,80,1024]{3,2,0,1:T(8,128)(2,1)}, bf16[3,1,80,1024]{3,2,0,1:T(8,128)(2,1)S(1)}, u32[]{:S(2)}, u32[]{:S(2)}) collective-permute-start(bf16[3,1,80,1024]{3,2,0,1:T(8,128)(2,1)} %get-tuple-element.501), channel_id=1, source_target_pairs={{0,64},{64,128},{128,192},{192,256},{256,320},{320,384},{384,448},... | collective-permute-start | bytes 1474568 | tf_op jit(solution)/shard_map/while/body/eval_jaxpr/ppermute | solution.py:34
  444.3 6.0 %collective-permute-done = bf16[3,1,80,1024]{3,2,0,1:T(8,128)(2,1)S(1)} collective-permute-done((bf16[3,1,80,1024]{3,2,0,1:T(8,128)(2,1)}, bf16[3,1,80,1024]{3,2,0,1:T(8,128)(2,1)S(1)}, u32[]{:S(2)}, u32[]{:S(2)}) %collective-permute-start) | collective-permute-done | bytes 491552 | tf_op jit(solution)/shard_map/while/body/eval_jaxpr/ppermute | solution.py:34
  450.4 1.4 conditional.2
  451.8 1.3 select_dynamic-update-slice_fusion.2
  453.8 73.5 %all-gather = bf16[24,2,1024]{2,1,0:T(2,128)(2,1)S(1)} all-gather(bf16[3,2,1024]{2,1,0:T(2,128)(2,1)S(1)} %copy.69), channel_id=2, replica_groups=mesh['section'=8,'dp'=64] {'section'}, dimensions={0}, use_global_device_ids=true | all-gather | bytes 110592 | tf_op jit(solution)/shard_map/all_gather | solution.py:38
  (122 shorter events, 38.2 us)
Async XLA Ops:
  0.6 529.0 %copy-start = (bf16[1024,125]{1,0:T(8,128)(2,1)S(1)}, bf16[1024,125]{1,0:T(8,128)(2,1)}, u32[]{:S(2)}) copy-start(bf16[1024,125]{1,0:T(8,128)(2,1)} %param.19) | copy-start | bytes 768004
  7.4 193.8 %all-to-all-start = ((bf16[64,16,4096]{2,1,0:T(8,128)(2,1)}), bf16[64,16,4096]{2,1,0:T(8,128)(2,1)}, u32[]{:S(2)}, u32[]{:S(2)}) async-start(bf16[64,16,4096]{2,1,0:T(8,128)(2,1)} %stack.2), calls=%async_computation | async-start | bytes 16777216 | tf_op jit(solution)/shard_map/all_to_all | solution.py:16
  220.0 2.8 copy-start.5
  222.7 21.1 %collective-permute-start = (bf16[3,1,80,1024]{3,2,0,1:T(8,128)(2,1)}, bf16[3,1,80,1024]{3,2,0,1:T(8,128)(2,1)S(1)}, u32[]{:S(2)}, u32[]{:S(2)}) collective-permute-start(bf16[3,1,80,1024]{3,2,0,1:T(8,128)(2,1)} %get-tuple-element.501), channel_id=1, source_target_pairs={{0,64},{64,128},{128,192},{192,256},{256,320},{320,384},{384,448},... | collective-permute-start | bytes 1474568 | tf_op jit(solution)/shard_map/while/body/eval_jaxpr/ppermute | solution.py:34
  246.5 11.3 %collective-permute-start = (bf16[3,1,80,1024]{3,2,0,1:T(8,128)(2,1)}, bf16[3,1,80,1024]{3,2,0,1:T(8,128)(2,1)S(1)}, u32[]{:S(2)}, u32[]{:S(2)}) collective-permute-start(bf16[3,1,80,1024]{3,2,0,1:T(8,128)(2,1)} %get-tuple-element.501), channel_id=1, source_target_pairs={{0,64},{64,128},{128,192},{192,256},{256,320},{320,384},{384,448},... | collective-permute-start | bytes 1474568 | tf_op jit(solution)/shard_map/while/body/eval_jaxpr/ppermute | solution.py:34
  259.0 1.9 copy-start.1
  259.2 3.8 copy-start.6
  266.1 3.7 copy-start.3
  269.9 1.9 copy-start.2
  271.7 2.0 copy-start.4
  282.4 12.5 %collective-permute-start = (bf16[3,1,80,1024]{3,2,0,1:T(8,128)(2,1)}, bf16[3,1,80,1024]{3,2,0,1:T(8,128)(2,1)S(1)}, u32[]{:S(2)}, u32[]{:S(2)}) collective-permute-start(bf16[3,1,80,1024]{3,2,0,1:T(8,128)(2,1)} %get-tuple-element.501), channel_id=1, source_target_pairs={{0,64},{64,128},{128,192},{192,256},{256,320},{320,384},{384,448},... | collective-permute-start | bytes 1474568 | tf_op jit(solution)/shard_map/while/body/eval_jaxpr/ppermute | solution.py:34
  296.1 1.9 copy-start.1
  296.3 3.8 copy-start.6
  303.2 3.7 copy-start.3
  306.9 1.9 copy-start.2
  308.8 2.0 copy-start.4
  319.5 11.3 %collective-permute-start = (bf16[3,1,80,1024]{3,2,0,1:T(8,128)(2,1)}, bf16[3,1,80,1024]{3,2,0,1:T(8,128)(2,1)S(1)}, u32[]{:S(2)}, u32[]{:S(2)}) collective-permute-start(bf16[3,1,80,1024]{3,2,0,1:T(8,128)(2,1)} %get-tuple-element.501), channel_id=1, source_target_pairs={{0,64},{64,128},{128,192},{192,256},{256,320},{320,384},{384,448},... | collective-permute-start | bytes 1474568 | tf_op jit(solution)/shard_map/while/body/eval_jaxpr/ppermute | solution.py:34
  333.5 33.1 %collective-permute-start = (bf16[3,1,80,1024]{3,2,0,1:T(8,128)(2,1)}, bf16[3,1,80,1024]{3,2,0,1:T(8,128)(2,1)S(1)}, u32[]{:S(2)}, u32[]{:S(2)}) collective-permute-start(bf16[3,1,80,1024]{3,2,0,1:T(8,128)(2,1)} %get-tuple-element.501), channel_id=1, source_target_pairs={{0,64},{64,128},{128,192},{192,256},{256,320},{320,384},{384,448},... | collective-permute-start | bytes 1474568 | tf_op jit(solution)/shard_map/while/body/eval_jaxpr/ppermute | solution.py:34
  369.3 11.2 %collective-permute-start = (bf16[3,1,80,1024]{3,2,0,1:T(8,128)(2,1)}, bf16[3,1,80,1024]{3,2,0,1:T(8,128)(2,1)S(1)}, u32[]{:S(2)}, u32[]{:S(2)}) collective-permute-start(bf16[3,1,80,1024]{3,2,0,1:T(8,128)(2,1)} %get-tuple-element.501), channel_id=1, source_target_pairs={{0,64},{64,128},{128,192},{192,256},{256,320},{320,384},{384,448},... | collective-permute-start | bytes 1474568 | tf_op jit(solution)/shard_map/while/body/eval_jaxpr/ppermute | solution.py:34
  383.3 18.1 %collective-permute-start = (bf16[3,1,80,1024]{3,2,0,1:T(8,128)(2,1)}, bf16[3,1,80,1024]{3,2,0,1:T(8,128)(2,1)S(1)}, u32[]{:S(2)}, u32[]{:S(2)}) collective-permute-start(bf16[3,1,80,1024]{3,2,0,1:T(8,128)(2,1)} %get-tuple-element.501), channel_id=1, source_target_pairs={{0,64},{64,128},{128,192},{192,256},{256,320},{320,384},{384,448},... | collective-permute-start | bytes 1474568 | tf_op jit(solution)/shard_map/while/body/eval_jaxpr/ppermute | solution.py:34
  404.2 11.2 %collective-permute-start = (bf16[3,1,80,1024]{3,2,0,1:T(8,128)(2,1)}, bf16[3,1,80,1024]{3,2,0,1:T(8,128)(2,1)S(1)}, u32[]{:S(2)}, u32[]{:S(2)}) collective-permute-start(bf16[3,1,80,1024]{3,2,0,1:T(8,128)(2,1)} %get-tuple-element.501), channel_id=1, source_target_pairs={{0,64},{64,128},{128,192},{192,256},{256,320},{320,384},{384,448},... | collective-permute-start | bytes 1474568 | tf_op jit(solution)/shard_map/while/body/eval_jaxpr/ppermute | solution.py:34
  418.1 32.2 %collective-permute-start = (bf16[3,1,80,1024]{3,2,0,1:T(8,128)(2,1)}, bf16[3,1,80,1024]{3,2,0,1:T(8,128)(2,1)S(1)}, u32[]{:S(2)}, u32[]{:S(2)}) collective-permute-start(bf16[3,1,80,1024]{3,2,0,1:T(8,128)(2,1)} %get-tuple-element.501), channel_id=1, source_target_pairs={{0,64},{64,128},{128,192},{192,256},{256,320},{320,384},{384,448},... | collective-permute-start | bytes 1474568 | tf_op jit(solution)/shard_map/while/body/eval_jaxpr/ppermute | solution.py:34
